TPU v7x, 32 devices: a whole 2x2x4 slice. The times are simulated.
32 devices in a mesh: row: 4 (over x, core), col: 4 (over z), depth: 2 (over y).
Axes of the slice: x: 2, y: 2, z: 4, core: 2. Of those that a mesh axis runs over, the one named last changes fastest.
Arguments:
- tokens: bfloat16 [512, 4096], P(('col', 'depth'), 'row'), may hold values from -6 to 6
- w_gate: bfloat16 [4096, 14336], P('row', 'col'), may hold values from -0.09375 to 0.09375
- w_up: bfloat16 [4096, 14336], P('row', 'col'), may hold values from -0.09375 to 0.09375
- w_down: bfloat16 [14336, 4096], P('col', 'row'), may hold values from -0.046875 to 0.046875
- cotangent: bfloat16 [512, 4096], P(('col', 'depth'), 'row'), may hold values from -0.25 to 0.25
Outputs:
- mixed: bfloat16 [512, 4096], P(('col', 'depth'), 'row')
- grad_gate: bfloat16 [4096, 14336], P(('row', 'depth'), 'col')
- grad_up: bfloat16 [4096, 14336], P(('row', 'depth'), 'col')
- grad_down: bfloat16 [14336, 4096], P(('col', 'depth'), 'row')
All inputs are finite; a program needn't handle non-finite values.
Results may differ from a plain program's by a relative error of at most 0.025.
Values may be sent and summed in bfloat16 or wider, within the bound.
No kernel may reach another device: no remote copies, remote signals or barrier semaphores. Data moves between devices by JAX's collectives and lax.ppermute only.
A program may use at most 128 MiB of HBM per device.

v0:
```python
import jax
import jax.numpy as jnp
from jax import lax
from jax.sharding import PartitionSpec as P

COLS_CONTRACT = (((1,), (1,)), ((), ()))
ROWS_CONTRACT = (((0,), (0,)), ((), ()))


def gate_grads(hidden_grad, gate_sum, up_sum):
    sigmoid_gate = jax.nn.sigmoid(gate_sum)
    d_gate = (hidden_grad * up_sum * sigmoid_gate * (1.0 + gate_sum * (1.0 - sigmoid_gate))).astype(
        jnp.bfloat16
    )
    d_up = (hidden_grad * gate_sum * sigmoid_gate).astype(jnp.bfloat16)
    return (d_gate, d_up)


def per_device(tokens, w_gate, w_up, w_down, cotangent):
    hid_width = w_gate.shape[1]
    token_rows = lax.all_gather(tokens, "col", axis=0, tiled=True)
    row_piece = token_rows
    joined = lax.psum_scatter(
        jnp.concatenate(
            [
                jnp.dot(row_piece, w_gate, preferred_element_type=jnp.float32),
                jnp.dot(row_piece, w_up, preferred_element_type=jnp.float32),
            ],
            axis=1,
        ).astype(jnp.bfloat16),
        "row",
        scatter_dimension=0,
        tiled=True,
    ).astype(jnp.float32)
    gate_sum = joined[:, :hid_width]
    up_sum = joined[:, hid_width:]
    hidden = (jax.nn.silu(gate_sum) * up_sum).astype(jnp.bfloat16)
    hidden_rows = lax.all_gather(hidden, "row", axis=0, tiled=True)
    row_piece = hidden_rows
    mixed = lax.psum_scatter(
        jnp.dot(row_piece, w_down, preferred_element_type=jnp.float32).astype(jnp.bfloat16),
        "col",
        scatter_dimension=0,
        tiled=True,
    )
    cot_rows = lax.all_gather(cotangent, "col", axis=0, tiled=True)
    row_piece = cot_rows
    hidden_grad = lax.psum_scatter(
        lax.dot_general(
            row_piece, w_down, COLS_CONTRACT, preferred_element_type=jnp.float32
        ).astype(jnp.bfloat16),
        "row",
        scatter_dimension=0,
        tiled=True,
    ).astype(jnp.float32)
    d_gate, d_up = gate_grads(hidden_grad, gate_sum, up_sum)
    d_gate_rows, d_up_rows = (
        lax.all_gather(d_gate, "row", axis=0, tiled=True),
        lax.all_gather(d_up, "row", axis=0, tiled=True),
    )
    down_term = lax.dot_general(
        hidden_rows, cot_rows, ROWS_CONTRACT, preferred_element_type=jnp.float32
    )
    grad_down = lax.psum_scatter(
        down_term.astype(jnp.bfloat16), "depth", scatter_dimension=0, tiled=True
    )
    layer_tokens = lax.all_to_all(token_rows, "depth", split_axis=1, concat_axis=0, tiled=True)
    block_rows = token_rows.shape[0]
    empty_grad = jnp.zeros((layer_tokens.shape[1], d_gate_rows.shape[1]), jnp.float32)
    first_row = jnp.int32(0)
    gate_total = empty_grad
    up_total = empty_grad
    gate_piece = lax.all_gather(d_gate_rows, "depth", axis=0, tiled=True)
    up_piece = lax.all_gather(d_up_rows, "depth", axis=0, tiled=True)
    for sub_index in range(gate_piece.shape[0] // block_rows):
        gate_block = gate_piece[sub_index * block_rows : (sub_index + 1) * block_rows]
        up_block = up_piece[sub_index * block_rows : (sub_index + 1) * block_rows]
        offset = first_row + sub_index * block_rows
        tok_block = lax.dynamic_slice_in_dim(layer_tokens, offset, block_rows, 0)
        gate_part = lax.optimization_barrier(
            lax.dot_general(
                tok_block, gate_block, ROWS_CONTRACT, preferred_element_type=jnp.float32
            ).astype(jnp.bfloat16)
        )
        up_part = lax.optimization_barrier(
            lax.dot_general(
                tok_block, up_block, ROWS_CONTRACT, preferred_element_type=jnp.float32
            ).astype(jnp.bfloat16)
        )
        gate_total = gate_total + gate_part.astype(jnp.float32)
        up_total = up_total + up_part.astype(jnp.float32)
    return (mixed, gate_total.astype(jnp.bfloat16), up_total.astype(jnp.bfloat16), grad_down)


def solution(mesh):
    placed = (
        P(("col", "depth"), "row"),
        P("row", "col"),
        P("row", "col"),
        P("col", "row"),
        P(("col", "depth"), "row"),
    )
    return jax.shard_map(
        per_device,
        mesh=mesh,
        in_specs=placed,
        out_specs=(
            P(("col", "depth"), "row"),
            P(("row", "depth"), "col"),
            P(("row", "depth"), "col"),
            P(("col", "depth"), "row"),
        ),
        check_vma=False,
    )
```

profile of v0, /device:TPU:0, one launch (start us, length us, event | category | flops | bytes accessed | tf_op | source)
XLA Modules:
  0.0 411.8 jit_solution(894660631228663583)
XLA Ops:
  7.2 17.7 %all_gather.21 = bf16[256,1024]{1,0:T(8,128)(2,1)S(1)} all-gather(bf16[64,1024]{1,0:T(8,128)(2,1)} %param.5), channel_id=1, replica_groups=mesh['row'=4,'col'=4,'depth'=2] {'col'}, dimensions={0}, use_global_device_ids=true | all-gather | bytes 655360 | tf_op jit(solution)/shard_map/all_gather | solution.py:21
  24.9 5.3 %convolution_convert_fusion.6 = bf16[256,3584]{1,0:T(8,128)(2,1)S(1)} fusion(bf16[256,1024]{1,0:T(8,128)(2,1)S(1)} %all_gather.21, bf16[1024,3584]{1,0:T(8,128)(2,1)} %param.7), kind=kOutput, calls=%fused_computation.12 | convolution fusion | flops 1879965696 | bytes 9699328 | tf_op jit(solution)/shard_map/dot_general | solution.py:27
  32.4 2.3 pad_maximum_fusion
  35.5 16.2 %all_gather.23 = bf16[256,1024]{1,0:T(8,128)(2,1)S(1)} all-gather(bf16[64,1024]{1,0:T(8,128)(2,1)S(1)} %copy-done.3), channel_id=1, replica_groups=mesh['row'=4,'col'=4,'depth'=2] {'col'}, dimensions={0}, use_global_device_ids=true | all-gather | bytes 655360 | tf_op jit(solution)/shard_map/all_gather | solution.py:46
  51.8 6.5 %convolution_convert_fusion.5 = bf16[256,3584]{1,0:T(8,128)(2,1)} fusion(bf16[256,1024]{1,0:T(8,128)(2,1)S(1)} %all_gather.23, bf16[3584,1024]{1,0:T(8,128)(2,1)} %param.8), kind=kOutput, calls=%fused_computation.11 | convolution fusion | flops 1879965696 | bytes 9699328 | tf_op jit(solution)/shard_map/dot_general | solution.py:49
  58.3 19.4 %reduce-scatter.5.cloned.1.call-done = bf16[64,7168]{1,0:T(8,128)(2,1)} async-done(((bf16[256,7168]{1,0:T(8,128)(2,1)}), bf16[64,7168]{1,0:T(8,128)(2,1)}) %reduce-scatter.5.cloned.1.call-update) | async-done | bytes 917520 | tf_op jit(solution)/shard_map/reduce_scatter | solution.py:23
  79.1 31.5 %reduce-scatter.9.cloned.1.call-done = bf16[64,3584]{1,0:T(8,128)(2,1)} async-done(((bf16[256,3584]{1,0:T(8,128)(2,1)}), bf16[64,3584]{1,0:T(8,128)(2,1)}) %reduce-scatter.9.cloned.1.call-update) | async-done | bytes 458768 | tf_op jit(solution)/shard_map/reduce_scatter | solution.py:48
  110.5 2.5 fusion.12
  114.3 20.0 %all-gather.8.cloned.1.call-done = bf16[256,3584]{1,0:T(8,128)(2,1)} async-done(((bf16[64,3584]{1,0:T(8,128)(2,1)}), bf16[256,3584]{1,0:T(8,128)(2,1)}) %all-gather.8.cloned.1.call-update) | async-done | bytes 1835024 | tf_op jit(solution)/shard_map/all_gather | solution.py:58
  134.4 23.1 %all-gather.12.cloned.1.call-done = bf16[256,3584]{1,0:T(8,128)(2,1)} async-done(((bf16[64,3584]{1,0:T(8,128)(2,1)}), bf16[256,3584]{1,0:T(8,128)(2,1)}) %all-gather.12.cloned.1.call-update) | async-done | bytes 1835024 | tf_op jit(solution)/shard_map/all_gather | solution.py:59
  157.5 23.0 %all-gather.6.cloned.1.call-done = bf16[256,3584]{1,0:T(8,128)(2,1)} async-done(((bf16[64,3584]{1,0:T(8,128)(2,1)}), bf16[256,3584]{1,0:T(8,128)(2,1)}) %all-gather.6.cloned.1.call-update) | async-done | bytes 1835024 | tf_op jit(solution)/shard_map/all_gather | solution.py:38
  180.6 6.6 %convolution_convert_fusion.8 = bf16[256,1024]{1,0:T(8,128)(2,1)} fusion(bf16[256,3584]{1,0:T(8,128)(2,1)} %all-gather.6.cloned.1.call-done, bf16[3584,1024]{1,0:T(8,128)(2,1)} %param.8), kind=kOutput, calls=%fused_computation.19 | convolution fusion | flops 1879310336 | bytes 9699328 | tf_op jit(solution)/shard_map/dot_general | solution.py:41
  187.3 5.3 %convolution_convert_fusion = bf16[3584,1024]{1,0:T(8,128)(2,1)} fusion(bf16[256,3584]{1,0:T(8,128)(2,1)S(1)} %copy-done.2, bf16[256,1024]{1,0:T(8,128)(2,1)S(1)} %all_gather.23), kind=kOutput, calls=%fused_computation | convolution fusion | flops 1882718208 | bytes 9699328 | tf_op jit(solution)/shard_map/dot_general | solution.py:61
  192.9 17.3 %all_to_all.16 = bf16[256,2,512]{0,2,1:T(8,128)(2,1)S(1)} all-to-all(bf16[256,2,512]{0,2,1:T(8,128)(2,1)S(1)} %bitcast.36), channel_id=1, replica_groups=mesh['row'=4,'col'=4,'depth'=2] {'depth'}, dimensions={1} | all-to-all | bytes 1048576 | tf_op jit(solution)/shard_map/all_to_all | solution.py:67
  210.2 28.3 %all-gather.10.cloned.1.call-done = bf16[512,3584]{1,0:T(8,128)(2,1)} async-done(((bf16[256,3584]{1,0:T(8,128)(2,1)}), bf16[512,3584]{1,0:T(8,128)(2,1)}) %all-gather.10.cloned.1.call-update) | async-done | bytes 3670032 | tf_op jit(solution)/shard_map/all_gather | solution.py:73
  238.4 2.8 fusion
  242.5 2.9 add_convert_fusion.1
  245.3 6.1 %copy.21 = bf16[512,3584]{1,0:T(8,128)(2,1)} copy(bf16[512,3584]{0,1:T(8,128)(2,1)} %add_convert_fusion.1) | data formatting | bytes 7340032
  251.5 39.4 %all-gather.14.cloned.1.call-done = bf16[512,3584]{1,0:T(8,128)(2,1)} async-done(((bf16[256,3584]{1,0:T(8,128)(2,1)}), bf16[512,3584]{1,0:T(8,128)(2,1)}) %all-gather.14.cloned.1.call-update) | async-done | bytes 3670032 | tf_op jit(solution)/shard_map/all_gather | solution.py:74
  290.8 2.8 fusion.2
  294.9 3.0 add_convert_fusion
  297.8 5.9 %copy.22 = bf16[512,3584]{1,0:T(8,128)(2,1)} copy(bf16[512,3584]{0,1:T(8,128)(2,1)} %add_convert_fusion) | data formatting | bytes 7340032
  303.7 11.8 %reduce-scatter.7.cloned.1.call-done = bf16[64,1024]{1,0:T(8,128)(2,1)} async-done(((bf16[256,1024]{1,0:T(8,128)(2,1)}), bf16[64,1024]{1,0:T(8,128)(2,1)}) %reduce-scatter.7.cloned.1.call-update) | async-done | bytes 131088 | tf_op jit(solution)/shard_map/reduce_scatter | solution.py:40
  315.5 89.7 %reduce-scatter.11.cloned.1.call-done = bf16[1792,1024]{1,0:T(8,128)(2,1)} async-done(((bf16[3584,1024]{1,0:T(8,128)(2,1)}), bf16[1792,1024]{1,0:T(8,128)(2,1)}) %reduce-scatter.11.cloned.1.call-update) | async-done | bytes 3670032 | tf_op jit(solution)/shard_map/reduce_scatter | solution.py:64
  (36 shorter events, 8.3 us)
Async XLA Ops:
  7.2 70.6 %reduce-scatter.5.cloned.1.call-start = ((), (), s32[]{:S(2)}) async-start(), calls=%async_computation.5 | async-start | bytes 4587520 | tf_op jit(solution)/shard_map/reduce_scatter | solution.py:23
  7.2 23.0 %slice-start = ((s8[7340032]{0:T(1024)(128)(4,1)}), s8[4194304]{0:T(1024)(128)(4,1)S(1)}, s32[]{:S(2)}) async-start(s8[7340032]{0:T(1024)(128)(4,1)} %bitcast.37), calls=%async_computation.14 | async-start | bytes 8388608
  24.9 5.3 %slice-start.1 = ((s8[7340032]{0:T(1024)(128)(4,1)}), s8[3145728]{0:T(1024)(128)(4,1)S(1)}, s32[]{:S(2)}) async-start(s8[7340032]{0:T(1024)(128)(4,1)} %bitcast.37), calls=%async_computation.15 | async-start | bytes 6291456
  34.6 0.9 copy-start.3
  34.6 75.9 %reduce-scatter.9.cloned.1.call-start = ((), (), s32[]{:S(2)}) async-start(), calls=%async_computation.8 | async-start | bytes 2293760 | tf_op jit(solution)/shard_map/reduce_scatter | solution.py:48
  58.3 76.1 %all-gather.8.cloned.1.call-start = ((), (), s32[]{:S(2)}) async-start(), calls=%async_computation.9 | async-start | bytes 2293760 | tf_op jit(solution)/shard_map/all_gather | solution.py:58
  113.1 44.4 %all-gather.12.cloned.1.call-start = ((), (), s32[]{:S(2)}) async-start(), calls=%async_computation.11 | async-start | bytes 2293760 | tf_op jit(solution)/shard_map/all_gather | solution.py:59
  113.7 66.9 %all-gather.6.cloned.1.call-start = ((), (), s32[]{:S(2)}) async-start(), calls=%async_computation.6 | async-start | bytes 2293760 | tf_op jit(solution)/shard_map/all_gather | solution.py:38
  114.3 124.2 %all-gather.10.cloned.1.call-start = ((), (), s32[]{:S(2)}) async-start(), calls=%async_computation.10 | async-start | bytes 5505024 | tf_op jit(solution)/shard_map/all_gather | solution.py:73
  134.4 156.5 %all-gather.14.cloned.1.call-start = ((), (), s32[]{:S(2)}) async-start(), calls=%async_computation.12 | async-start | bytes 5505024 | tf_op jit(solution)/shard_map/all_gather | solution.py:74
  157.5 158.1 %reduce-scatter.7.cloned.1.call-start = ((), (), s32[]{:S(2)}) async-start(), calls=%async_computation.7 | async-start | bytes 655360 | tf_op jit(solution)/shard_map/reduce_scatter | solution.py:40
  180.6 6.7 %copy-start.2 = (bf16[256,3584]{1,0:T(8,128)(2,1)S(1)}, bf16[256,3584]{1,0:T(8,128)(2,1)}, u32[]{:S(2)}) copy-start(bf16[256,3584]{1,0:T(8,128)(2,1)} %all-gather.6.cloned.1.call-done) | copy-start | bytes 5505028
  187.2 218.0 %reduce-scatter.11.cloned.1.call-start = ((), (), s32[]{:S(2)}) async-start(), calls=%async_computation.13 | async-start | bytes 11010048 | tf_op jit(solution)/shard_map/reduce_scatter | solution.py:64
  238.4 2.8 copy-start
  290.8 2.8 copy-start.1
Sparse Core Ops, SparseCore 0:
  34.8 42.9 reduce-scatter.4
  80.9 29.6 reduce-scatter.8
  113.2 21.0 all-gather.7
  136.3 21.0 all-gather.11
  159.4 21.0 all-gather.5
  182.0 56.4 all-gather.9
  240.0 50.8 all-gather.13
  293.7 21.8 reduce-scatter.6
  318.4 86.7 reduce-scatter.10
where the time goes:
time: 412 us
  waiting for transfers between devices  287 us (70%)
  blocking collectives  51.3 us (12%)
  matrix products  33.8 us (8%)
  between operations  14 us (3%)
  local copies, waits for them, and re-layouts  13.1 us (3%)
  other arithmetic  11.9 us (3%)
    reduce_scatter x1, waiting for transfers between devices, per_device(): lax.psum_scatter(down_term.astype(jnp.bfloat16), 'depth', scatter_dimensi...  89.7 us
    all_gather x1, waiting for transfers between devices, per_device(): up_piece = lax.all_gather(d_up_rows, 'depth', axis=0, tiled=True)  39.4 us
    reduce_scatter x1, waiting for transfers between devices, per_device(): lax.psum_scatter(lax.dot_general(row_piece, w_down, COLS_CONTRACT, prefer...  31.5 us
    all_gather x1, waiting for transfers between devices, per_device(): gate_piece = lax.all_gather(d_gate_rows, 'depth', axis=0, tiled=True)  28.3 us
    all_gather x1, waiting for transfers between devices, per_device(): lax.all_gather(d_up, 'row', axis=0, tiled=True)  23.1 us
    all_gather x1, waiting for transfers between devices, per_device(): hidden_rows = lax.all_gather(hidden, 'row', axis=0, tiled=True)  23 us
    all_gather x1, waiting for transfers between devices, per_device(): lax.all_gather(d_gate, 'row', axis=0, tiled=True)  20 us
    reduce_scatter x1, waiting for transfers between devices, per_device(): lax.psum_scatter(jnp.concatenate([jnp.dot(row_piece, w_gate, preferred_el...  19.4 us
  transfers between devices with their start and end apart: 9, of which 9 were waited for; matrix products, arithmetic and copies ran while one was open for 11% of the time, Pallas kernels for 0%

commit v1 on v0

--- a/solution.py
+++ b/solution.py
@@ -3,6 +3,7 @@
 from jax import lax
 from jax.sharding import PartitionSpec as P
 
+
 COLS_CONTRACT = (((1,), (1,)), ((), ()))
 ROWS_CONTRACT = (((0,), (0,)), ((), ()))
 
@@ -16,7 +17,7 @@
     return (d_gate, d_up)
 
 
-def per_device(tokens, w_gate, w_up, w_down, cotangent):
+def gathered(tokens, w_gate, w_up, w_down, cotangent):
     hid_width = w_gate.shape[1]
     token_rows = lax.all_gather(tokens, "col", axis=0, tiled=True)
     row_piece = token_rows
@@ -92,7 +93,117 @@
     return (mixed, gate_total.astype(jnp.bfloat16), up_total.astype(jnp.bfloat16), grad_down)
 
 
+def swap(value, axis, size, step):
+    return lax.ppermute(value, axis, [(at, (at + step) % size) for at in range(size)])
+
+
+def partner(value, size, bit):
+    return lax.ppermute(value, "row", [(at, at ^ bit) for at in range(size)])
+
+
+def bf16_dot(left, right, dims):
+    return lax.dot_general(left, right, dims, preferred_element_type=jnp.float32).astype(
+        jnp.bfloat16
+    )
+
+
+MATMUL = (((1,), (0,)), ((), ()))
+
+
+def paired(tokens, w_gate, w_up, w_down, cotangent):
+    n_row, n_col, n_depth = (lax.axis_size(name) for name in ("row", "col", "depth"))
+    depth = lax.axis_index("depth")
+    even = lax.axis_index("row") % 2 == 0
+    first = depth == 0
+    rows, feats = tokens.shape
+    half = w_gate.shape[1] // n_depth
+
+    own = jnp.stack([tokens, cotangent])
+    other = swap(own, "depth", n_depth, 1)
+    pair = {
+        0: jnp.concatenate([jnp.where(even, own, other), jnp.where(even, other, own)], axis=1)
+    }
+    groups = [0]
+    for step in range(1, n_col):
+        near, back = (step + 1) // 2, step % 2 == 0
+        at = n_col - near if back else near
+        source = (at + 1) % n_col if back else at - 1
+        pair[at] = [swap(pair[source][part], "col", n_col, -1 if back else 1) for part in range(2)]
+        groups.append(at)
+
+    my_gate, my_up = lax.optimization_barrier(
+        (
+            lax.dynamic_slice_in_dim(w_gate, depth * half, half, 1),
+            lax.dynamic_slice_in_dim(w_up, depth * half, half, 1),
+        )
+    )
+    my_down = lax.dynamic_slice_in_dim(w_down, depth * half, half, 0)
+
+    mixed = None
+    hidden_all, tok_all, cot_all, grads_all = [], [], [], []
+    for at in groups:
+        tok, cot = pair[at][0], pair[at][1]
+        tok_all.append(tok)
+        cot_all.append(cot)
+        inner = [bf16_dot(tok, my_gate, MATMUL), bf16_dot(tok, my_up, MATMUL)]
+        mine = jnp.stack([term[:rows] for term in inner])
+        rest = partner(jnp.stack([term[rows:] for term in inner]), n_row, 1)
+        mine = mine + rest
+        sums = mine.astype(jnp.float32) + partner(mine, n_row, 2).astype(jnp.float32)
+        gate_sum, up_sum = sums[0], sums[1]
+        back = bf16_dot(cot, my_down, COLS_CONTRACT)
+        rest = partner(back[rows:], n_row, 1)
+        mine = back[:rows] + rest
+        hidden_grad = mine.astype(jnp.float32) + partner(mine, n_row, 2).astype(jnp.float32)
+        hidden = (jax.nn.silu(gate_sum) * up_sum).astype(jnp.bfloat16)
+        d_gate, d_up = gate_grads(hidden_grad, gate_sum, up_sum)
+        grads = jnp.stack([d_gate, d_up])
+        across = swap(grads, "depth", n_depth, 1)
+        beside = partner(jnp.stack([d_gate, d_up, hidden]), n_row, 1)
+
+        hidden_rows = jnp.concatenate([hidden, beside[2]], axis=0)
+        hidden_all.append(hidden_rows)
+        part = bf16_dot(hidden_rows, my_down, MATMUL)
+        low, high = part[:rows], part[rows:]
+        term = jnp.where(even, low, high).astype(jnp.float32) + swap(
+            jnp.where(even, high, low), "depth", n_depth, 1
+        ).astype(jnp.float32)
+        if at:
+            term = swap(term.astype(jnp.bfloat16), "col", n_col, -at).astype(jnp.float32)
+        mixed = term if mixed is None else mixed + term
+
+        near_cols = jnp.concatenate([grads, beside[:2]], axis=1)
+        far_cols = jnp.concatenate([partner(across, n_row, 1), across], axis=1)
+        grads_all.append(
+            jnp.concatenate(
+                [jnp.where(first, near_cols, far_cols), jnp.where(first, far_cols, near_cols)],
+                axis=2,
+            )
+        )
+
+    tok_all = jnp.concatenate(tok_all, axis=0)
+    cot_all = jnp.concatenate(cot_all, axis=0)
+    width = feats // n_depth
+    tok_part = lax.dynamic_slice_in_dim(tok_all, depth * width, width, 1)
+    grad_down = bf16_dot(jnp.concatenate(hidden_all, axis=0), cot_all, ROWS_CONTRACT)
+    gate_rows, up_rows, tok_part = lax.optimization_barrier(
+        (
+            jnp.concatenate([block[0] for block in grads_all], axis=0),
+            jnp.concatenate([block[1] for block in grads_all], axis=0),
+            tok_part,
+        )
+    )
+    grad_gate = bf16_dot(tok_part, gate_rows, ROWS_CONTRACT)
+    grad_up = bf16_dot(tok_part, up_rows, ROWS_CONTRACT)
+    return (mixed.astype(jnp.bfloat16), grad_gate, grad_up, grad_down)
+
+
 def solution(mesh):
+    fits = mesh.shape["row"] == 4 and mesh.shape["depth"] == 2
+
+    def per_device(*arrays):
+        return paired(*arrays) if fits else gathered(*arrays)
+
     placed = (
         P(("col", "depth"), "row"),
         P("row", "col"),

time: 412 us -> 172 us (0.42)
  waiting for transfers between devices: 287 us -> 89.1 us
  blocking collectives: 51.3 us -> 0 us
  starting transfers between devices: 0.36 us -> 37.1 us
  between operations: 14 us -> 1.62 us
  matrix products: 33.8 us -> 27.3 us
  local copies, waits for them, and re-layouts: 13.1 us -> 8.09 us
    reduce_scatter x4 -> x0, waiting for transfers between devices: 152 us -> none  [the longest x1 89.7 us: per_device(): lax.psum_scatter(down_term.astype(jnp.bfloat16), 'depth', scatter_dimensi...]
    all_gather x5 -> x0, waiting for transfers between devices: 134 us -> none  [the longest x1 39.4 us: per_device(): up_piece = lax.all_gather(d_up_rows, 'depth', axis=0, tiled=True)]
    ppermute x0 -> x42, waiting for transfers between devices: none -> 89.1 us  [the longest x18 48.6 us: swap(): lax.ppermute(value, axis, [(at, (at + step) % size) for at in range(size)])]
    ppermute x0 -> x42, starting transfers between devices: none -> 37.1 us  [the longest x18 25 us: swap(): lax.ppermute(value, axis, [(at, (at + step) % size) for at in range(size)])]
    all_gather x2 -> x0, blocking collectives: 33.9 us -> none  [the longest x1 17.7 us: per_device(): token_rows = lax.all_gather(tokens, 'col', axis=0, tiled=True)]
    all_to_all x1 -> x0, blocking collectives: 17.3 us -> none  [per_device(): lax.all_to_all(token_rows, 'depth', split_axis=1, concat_axis=0, tiled=True)]
    unnamed x14 -> x21, local copies, waits for them, and re-layouts: 12.9 us -> 0.78 us
    convert_element_type x4 -> x8, other arithmetic: 9.67 us -> 1.46 us  [the longest x1 0.78 us: paired(): return (mixed.astype(jnp.bfloat16), grad_gate, grad_up, grad_down)]
  transfers between devices with their start and end apart: 9 -> 42, of which waited for: 9 -> 15; matrix products, arithmetic and copies ran while one was open for 11% -> 24% of each run, Pallas kernels for 0% -> 0%
where the time goes in v1:
time: 172 us; the launch traced here: 171 us
  waiting for transfers between devices  89.1 us (52%)
  starting transfers between devices  37.1 us (22%)
  matrix products  27.3 us (16%)
  other arithmetic  8.18 us (5%)
  local copies, waits for them, and re-layouts  8.09 us (5%)
    ppermute x18, waiting for transfers between devices, swap(): lax.ppermute(value, axis, [(at, (at + step) % size) for at in range(size)])  48.6 us
    ppermute x24, waiting for transfers between devices, partner(): return lax.ppermute(value, 'row', [(at, at ^ bit) for at in range(size)])  40.5 us
    dot_general x19, matrix products, bf16_dot(): lax.dot_general(left, right, dims, preferred_element_type=jnp.float32)  27.3 us
    ppermute x18, starting transfers between devices, swap(): lax.ppermute(value, axis, [(at, (at + step) % size) for at in range(size)])  25 us
    ppermute x24, starting transfers between devices, partner(): return lax.ppermute(value, 'row', [(at, at ^ bit) for at in range(size)])  12.1 us
    dynamic_slice x1, local copies, waits for them, and re-layouts, paired(): lax.dynamic_slice_in_dim(w_up, depth * half, half, 1)  6.7 us
  transfers between devices with their start and end apart: 42, of which 15 were waited for; matrix products, arithmetic and copies ran while one was open for 24% of the time, Pallas kernels for 0%

profile of v1, /device:TPU:0, one launch (start us, length us, event | category | flops | bytes accessed | tf_op | source)
XLA Modules:
  0.0 171.4 jit_solution(18219350482995599522)
XLA Ops:
  1.6 3.1 %collective-permute-start = (bf16[2,64,1024]{2,1,0:T(8,128)(2,1)S(1)}, bf16[2,64,1024]{2,1,0:T(8,128)(2,1)S(1)}, u32[]{:S(2)}, u32[]{:S(2)}) collective-permute-start(bf16[2,64,1024]{2,1,0:T(8,128)(2,1)S(1)} %pad_maximum_fusion.23), channel_id=1, source_target_pairs={{0,1},{1,0},{2,3},{3,2},{4,5},{5,4},{6,7},{7,6},{8,9},{9,8},{10,11... | collective-permute-start | bytes 786440 | tf_op jit(solution)/shard_map/ppermute | solution.py:97
  4.7 6.7 %constant_dynamic-slice_fusion = (bf16[1024,1792]{1,0:T(8,128)(2,1)}, bf16[1024,1792]{1,0:T(8,128)(2,1)}) fusion(bf16[1024,3584]{1,0:T(8,128)(2,1)} %param.7, s32[]{:T(128)S(6)} %select_n.104, bf16[1024,3584]{1,0:T(8,128)(2,1)} %param.6), kind=kLoop, calls=%fused_computation.256 | loop fusion | bytes 14680068 | tf_op jit(solution)/shard_map/dynamic_slice | solution.py:137
  11.5 1.6 collective-permute-start.7
  13.1 2.2 %collective-permute-start.16 = (bf16[128,1024]{1,0:T(8,128)(2,1)S(1)}, bf16[128,1024]{1,0:T(8,128)(2,1)S(1)}, u32[]{:S(2)}, u32[]{:S(2)}) collective-permute-start(bf16[128,1024]{1,0:T(8,128)(2,1)S(1)} %get-tuple-element.47), channel_id=1, source_target_pairs={{0,6},{2,0},{4,2},{6,4},{1,7},{3,1},{5,3},{7,5},{8,14},{10,8},{12,... | collective-permute-start | bytes 786440 | tf_op jit(solution)/shard_map/ppermute | solution.py:97
  15.4 3.8 %collective-permute-start.19 = (bf16[128,1024]{1,0:T(8,128)(2,1)S(1)}, bf16[128,1024]{1,0:T(8,128)(2,1)S(1)}, u32[]{:S(2)}, u32[]{:S(2)}) collective-permute-start(bf16[128,1024]{1,0:T(8,128)(2,1)S(1)} %get-tuple-element.46), channel_id=1, source_target_pairs={{0,6},{2,0},{4,2},{6,4},{1,7},{3,1},{5,3},{7,5},{8,14},{10,8},{12,... | collective-permute-start | bytes 786440 | tf_op jit(solution)/shard_map/ppermute | solution.py:97
  19.2 2.8 %convolution_convert_fusion.13 = bf16[128,1792]{1,0:T(8,128)(2,1)S(1)} fusion(bf16[128,1024]{1,0:T(8,128)(2,1)S(1)} %get-tuple-element.47, bf16[1024,1792]{1,0:T(8,128)(2,1)} %get-tuple-element.10), kind=kOutput, calls=%fused_computation.15 | convolution fusion | flops 469991424 | bytes 4390912 | tf_op jit(solution)/shard_map/dot_general | solution.py:105
  26.5 1.6 collective-permute-start.4
  29.5 4.3 %collective-permute-done.10 = bf16[128,1024]{1,0:T(8,128)(2,1)S(1)} collective-permute-done((bf16[128,1024]{1,0:T(8,128)(2,1)S(1)}, bf16[128,1024]{1,0:T(8,128)(2,1)S(1)}, u32[]{:S(2)}, u32[]{:S(2)}) %collective-permute-start.10) | collective-permute-done | bytes 262176 | tf_op jit(solution)/shard_map/ppermute | solution.py:97
  41.7 10.8 %collective-permute-done.25 = bf16[128,1024]{1,0:T(8,128)(2,1)S(1)} collective-permute-done((bf16[128,1024]{1,0:T(8,128)(2,1)S(1)}, bf16[128,1024]{1,0:T(8,128)(2,1)S(1)}, u32[]{:S(2)}, u32[]{:S(2)}) %collective-permute-start.25) | collective-permute-done | bytes 262176 | tf_op jit(solution)/shard_map/ppermute | solution.py:97
  55.4 2.1 %collective-permute-done.28 = bf16[128,1024]{1,0:T(8,128)(2,1)S(1)} collective-permute-done((bf16[128,1024]{1,0:T(8,128)(2,1)S(1)}, bf16[128,1024]{1,0:T(8,128)(2,1)S(1)}, u32[]{:S(2)}, u32[]{:S(2)}) %collective-permute-start.28) | collective-permute-done | bytes 262176 | tf_op jit(solution)/shard_map/ppermute | solution.py:97
  57.5 1.5 collective-permute-start.12
  62.8 3.1 %collective-permute-done.2 = bf16[2,64,1792]{2,1,0:T(8,128)(2,1)S(1)} collective-permute-done((bf16[2,64,1792]{2,1,0:T(8,128)(2,1)S(1)}, bf16[2,64,1792]{2,1,0:T(8,128)(2,1)S(1)}, u32[]{:S(2)}, u32[]{:S(2)}) %collective-permute-start.2) | collective-permute-done | bytes 458784 | tf_op jit(solution)/shard_map/ppermute | solution.py:101
  68.8 1.6 collective-permute-start.30
  70.5 15.1 %collective-permute-done.9 = bf16[2,64,1792]{2,1,0:T(8,128)(2,1)S(1)} collective-permute-done((bf16[2,64,1792]{2,1,0:T(8,128)(2,1)S(1)}, bf16[2,64,1792]{2,1,0:T(8,128)(2,1)S(1)}, u32[]{:S(2)}, u32[]{:S(2)}) %collective-permute-start.9) | collective-permute-done | bytes 458784 | tf_op jit(solution)/shard_map/ppermute | solution.py:101
  85.9 9.5 %collective-permute-done.18 = bf16[2,64,1792]{2,1,0:T(8,128)(2,1)S(1)} collective-permute-done((bf16[2,64,1792]{2,1,0:T(8,128)(2,1)S(1)}, bf16[2,64,1792]{2,1,0:T(8,128)(2,1)S(1)}, u32[]{:S(2)}, u32[]{:S(2)}) %collective-permute-start.18) | collective-permute-done | bytes 458784 | tf_op jit(solution)/shard_map/ppermute | solution.py:101
  96.4 1.6 collective-permute-start.27
  98.9 9.1 %collective-permute-done.27 = bf16[2,64,1792]{2,1,0:T(8,128)(2,1)S(1)} collective-permute-done((bf16[2,64,1792]{2,1,0:T(8,128)(2,1)S(1)}, bf16[2,64,1792]{2,1,0:T(8,128)(2,1)S(1)}, u32[]{:S(2)}, u32[]{:S(2)}) %collective-permute-start.27) | collective-permute-done | bytes 458784 | tf_op jit(solution)/shard_map/ppermute | solution.py:101
  113.3 8.3 %collective-permute-done.38 = bf16[2,64,1792]{2,1,0:T(8,128)(2,1)S(1)} collective-permute-done((bf16[2,64,1792]{2,1,0:T(8,128)(2,1)S(1)}, bf16[2,64,1792]{2,1,0:T(8,128)(2,1)S(1)}, u32[]{:S(2)}, u32[]{:S(2)}) %collective-permute-start.38) | collective-permute-done | bytes 458784 | tf_op jit(solution)/shard_map/ppermute | solution.py:97
  125.5 18.1 %collective-permute-done.23 = bf16[64,1024]{1,0:T(8,128)(2,1)S(1)} collective-permute-done((bf16[64,1024]{1,0:T(8,128)(2,1)S(1)}, bf16[64,1024]{1,0:T(8,128)(2,1)S(1)}, u32[]{:S(2)}, u32[]{:S(2)}) %collective-permute-start.23) | collective-permute-done | bytes 131104 | tf_op jit(solution)/shard_map/ppermute | solution.py:97
  145.8 4.2 %collective-permute-done.14 = bf16[64,1024]{1,0:T(8,128)(2,1)S(1)} collective-permute-done((bf16[64,1024]{1,0:T(8,128)(2,1)S(1)}, bf16[64,1024]{1,0:T(8,128)(2,1)S(1)}, u32[]{:S(2)}, u32[]{:S(2)}) %collective-permute-start.14) | collective-permute-done | bytes 131104 | tf_op jit(solution)/shard_map/ppermute | solution.py:97
  150.5 4.1 %collective-permute-start.15 = (bf16[64,1024]{1,0:T(8,128)(2,1)S(1)}, bf16[64,1024]{1,0:T(8,128)(2,1)S(1)}, u32[]{:S(2)}, u32[]{:S(2)}) collective-permute-start(bf16[64,1024]{1,0:T(8,128)(2,1)S(1)} %add_convert_fusion.3), channel_id=1, source_target_pairs={{0,6},{2,0},{4,2},{6,4},{1,7},{3,1},{5,3},{7,5},{8,14},{10,8},{12,... | collective-permute-start | bytes 393224 | tf_op jit(solution)/shard_map/ppermute | solution.py:97
  156.8 3.9 %convolution_convert_fusion.2 = bf16[1792,1024]{1,0:T(8,128)(2,1)} fusion(bf16[512,1792]{1,0:T(8,128)(2,1)S(1)} %constant_dynamic-update-slice_fusion.8, bf16[128,1024]{1,0:T(8,128)(2,1)S(1)} %collective-permute-done.28, bf16[128,1024]{1,0:T(8,128)(2,1)S(1)} %collective-permute-done.19, bf16[128,1024]{1,0:T(8,128)(2,1)S(1)} %collective-permute-done.10, ...), kind=kOutput, calls=%fused_computation.2 | convolution fusion | flops 1885077504 | bytes 6553600 | tf_op jit(solution)/shard_map/dot_general | solution.py:105
  162.7 3.9 %convolution_convert_fusion.1 = bf16[512,3584]{1,0:T(8,128)(2,1)} fusion(bf16[512,512]{1,0:T(8,128)(2,1)S(1)} %fusion.29, bf16[512,3584]{1,0:T(8,128)(2,1)S(1)} %pad_maximum_fusion), kind=kOutput, calls=%fused_computation.1 | convolution fusion | flops 1880883200 | bytes 7864320 | tf_op jit(solution)/shard_map/dot_general | solution.py:105
  166.6 3.9 %convolution_convert_fusion = bf16[512,3584]{1,0:T(8,128)(2,1)} fusion(bf16[512,512]{1,0:T(8,128)(2,1)S(1)} %fusion.29, bf16[512,3584]{1,0:T(8,128)(2,1)S(1)} %pad_maximum_fusion.1), kind=kOutput, calls=%fused_computation | convolution fusion | flops 1880883200 | bytes 7864320 | tf_op jit(solution)/shard_map/dot_general | solution.py:105
  (186 shorter events, 42.9 us)
Async XLA Ops:
  11.5 15.0 %collective-permute-start.7 = (bf16[128,1024]{1,0:T(8,128)(2,1)S(1)}, bf16[128,1024]{1,0:T(8,128)(2,1)S(1)}, u32[]{:S(2)}, u32[]{:S(2)}) collective-permute-start(bf16[128,1024]{1,0:T(8,128)(2,1)S(1)} %get-tuple-element.47), channel_id=1, source_target_pairs={{0,2},{2,4},{4,6},{6,0},{1,3},{3,5},{5,7},{7,1},{8,10},{10,12},{12... | collective-permute-start | bytes 786440 | tf_op jit(solution)/shard_map/ppermute | solution.py:97
  13.1 22.1 %collective-permute-start.16 = (bf16[128,1024]{1,0:T(8,128)(2,1)S(1)}, bf16[128,1024]{1,0:T(8,128)(2,1)S(1)}, u32[]{:S(2)}, u32[]{:S(2)}) collective-permute-start(bf16[128,1024]{1,0:T(8,128)(2,1)S(1)} %get-tuple-element.47), channel_id=1, source_target_pairs={{0,6},{2,0},{4,2},{6,4},{1,7},{3,1},{5,3},{7,5},{8,14},{10,8},{12,... | collective-permute-start | bytes 786440 | tf_op jit(solution)/shard_map/ppermute | solution.py:97
  15.4 18.5 %collective-permute-start.10 = (bf16[128,1024]{1,0:T(8,128)(2,1)S(1)}, bf16[128,1024]{1,0:T(8,128)(2,1)S(1)}, u32[]{:S(2)}, u32[]{:S(2)}) collective-permute-start(bf16[128,1024]{1,0:T(8,128)(2,1)S(1)} %get-tuple-element.46), channel_id=1, source_target_pairs={{0,2},{2,4},{4,6},{6,0},{1,3},{3,5},{5,7},{7,1},{8,10},{10,12},{12... | collective-permute-start | bytes 786440 | tf_op jit(solution)/shard_map/ppermute | solution.py:97
  15.4 22.1 %collective-permute-start.19 = (bf16[128,1024]{1,0:T(8,128)(2,1)S(1)}, bf16[128,1024]{1,0:T(8,128)(2,1)S(1)}, u32[]{:S(2)}, u32[]{:S(2)}) collective-permute-start(bf16[128,1024]{1,0:T(8,128)(2,1)S(1)} %get-tuple-element.46), channel_id=1, source_target_pairs={{0,6},{2,0},{4,2},{6,4},{1,7},{3,1},{5,3},{7,5},{8,14},{10,8},{12,... | collective-permute-start | bytes 786440 | tf_op jit(solution)/shard_map/ppermute | solution.py:97
  26.5 41.2 %collective-permute-start.4 = (bf16[64,1792]{1,0:T(8,128)(2,1)S(1)}, bf16[64,1792]{1,0:T(8,128)(2,1)S(1)}, u32[]{:S(2)}, u32[]{:S(2)}) collective-permute-start(bf16[64,1792]{1,0:T(8,128)(2,1)S(1)} %slice_add_fusion.3), channel_id=1, source_target_pairs={{0,16},{8,24},{16,0},{24,8},{1,17},{9,25},{17,1},{25,9},{2,18},{10... | collective-permute-start | bytes 688136 | tf_op jit(solution)/shard_map/ppermute | solution.py:101
  33.9 26.6 %collective-permute-start.8 = (bf16[2,64,1792]{2,1,0:T(8,128)(2,1)S(1)}, bf16[2,64,1792]{2,1,0:T(8,128)(2,1)S(1)}, u32[]{:S(2)}, u32[]{:S(2)}) collective-permute-start(bf16[2,64,1792]{2,1,0:T(8,128)(2,1)S(1)} %pad_maximum_fusion.15), channel_id=1, source_target_pairs={{0,8},{8,0},{16,24},{24,16},{1,9},{9,1},{17,25},{25,17},{2,10},{10... | collective-permute-start | bytes 1376264 | tf_op jit(solution)/shard_map/ppermute | solution.py:101
  37.5 23.6 %collective-permute-start.17 = (bf16[2,64,1792]{2,1,0:T(8,128)(2,1)S(1)}, bf16[2,64,1792]{2,1,0:T(8,128)(2,1)S(1)}, u32[]{:S(2)}, u32[]{:S(2)}) collective-permute-start(bf16[2,64,1792]{2,1,0:T(8,128)(2,1)S(1)} %pad_maximum_fusion.16), channel_id=1, source_target_pairs={{0,8},{8,0},{16,24},{24,16},{1,9},{9,1},{17,25},{25,17},{2,10},{10... | collective-permute-start | bytes 1376264 | tf_op jit(solution)/shard_map/ppermute | solution.py:101
  40.7 16.7 %collective-permute-start.28 = (bf16[128,1024]{1,0:T(8,128)(2,1)S(1)}, bf16[128,1024]{1,0:T(8,128)(2,1)S(1)}, u32[]{:S(2)}, u32[]{:S(2)}) collective-permute-start(bf16[128,1024]{1,0:T(8,128)(2,1)S(1)} %collective-permute-done.10), channel_id=1, source_target_pairs={{0,2},{2,4},{4,6},{6,0},{1,3},{3,5},{5,7},{7,1},{8,10},{10,12},{12... | collective-permute-start | bytes 786440 | tf_op jit(solution)/shard_map/ppermute | solution.py:97
  57.5 39.0 %collective-permute-start.12 = (bf16[64,1792]{1,0:T(8,128)(2,1)S(1)}, bf16[64,1792]{1,0:T(8,128)(2,1)S(1)}, u32[]{:S(2)}, u32[]{:S(2)}) collective-permute-start(bf16[64,1792]{1,0:T(8,128)(2,1)S(1)} %slice_add_fusion.2), channel_id=1, source_target_pairs={{0,16},{8,24},{16,0},{24,8},{1,17},{9,25},{17,1},{25,9},{2,18},{10... | collective-permute-start | bytes 688136 | tf_op jit(solution)/shard_map/ppermute | solution.py:101
  60.4 38.0 %collective-permute-start.21 = (bf16[64,1792]{1,0:T(8,128)(2,1)S(1)}, bf16[64,1792]{1,0:T(8,128)(2,1)S(1)}, u32[]{:S(2)}, u32[]{:S(2)}) collective-permute-start(bf16[64,1792]{1,0:T(8,128)(2,1)S(1)} %slice_add_fusion.1), channel_id=1, source_target_pairs={{0,16},{8,24},{16,0},{24,8},{1,17},{9,25},{17,1},{25,9},{2,18},{10... | collective-permute-start | bytes 688136 | tf_op jit(solution)/shard_map/ppermute | solution.py:101
  65.9 19.7 %collective-permute-start.9 = (bf16[2,64,1792]{2,1,0:T(8,128)(2,1)S(1)}, bf16[2,64,1792]{2,1,0:T(8,128)(2,1)S(1)}, u32[]{:S(2)}, u32[]{:S(2)}) collective-permute-start(bf16[2,64,1792]{2,1,0:T(8,128)(2,1)S(1)} %maximum_add_fusion.1), channel_id=1, source_target_pairs={{0,16},{8,24},{16,0},{24,8},{1,17},{9,25},{17,1},{25,9},{2,18},{10... | collective-permute-start | bytes 1376264 | tf_op jit(solution)/shard_map/ppermute | solution.py:101
  67.7 27.7 %collective-permute-start.18 = (bf16[2,64,1792]{2,1,0:T(8,128)(2,1)S(1)}, bf16[2,64,1792]{2,1,0:T(8,128)(2,1)S(1)}, u32[]{:S(2)}, u32[]{:S(2)}) collective-permute-start(bf16[2,64,1792]{2,1,0:T(8,128)(2,1)S(1)} %maximum_add_fusion.2), channel_id=1, source_target_pairs={{0,16},{8,24},{16,0},{24,8},{1,17},{9,25},{17,1},{25,9},{2,18},{10... | collective-permute-start | bytes 1376264 | tf_op jit(solution)/shard_map/ppermute | solution.py:101
  68.8 39.3 %collective-permute-start.30 = (bf16[64,1792]{1,0:T(8,128)(2,1)S(1)}, bf16[64,1792]{1,0:T(8,128)(2,1)S(1)}, u32[]{:S(2)}, u32[]{:S(2)}) collective-permute-start(bf16[64,1792]{1,0:T(8,128)(2,1)S(1)} %slice_add_fusion), channel_id=1, source_target_pairs={{0,16},{8,24},{16,0},{24,8},{1,17},{9,25},{17,1},{25,9},{2,18},{10... | collective-permute-start | bytes 688136 | tf_op jit(solution)/shard_map/ppermute | solution.py:101
  85.6 25.3 %collective-permute-start.5 = (bf16[3,64,1792]{2,1,0:T(8,128)(2,1)S(1)}, bf16[3,64,1792]{2,1,0:T(8,128)(2,1)S(1)}, u32[]{:S(2)}, u32[]{:S(2)}) collective-permute-start(bf16[3,64,1792]{2,1,0:T(8,128)(2,1)S(1)} %pad_maximum_fusion.10), channel_id=1, source_target_pairs={{0,8},{8,0},{16,24},{24,16},{1,9},{9,1},{17,25},{25,17},{2,10},{10... | collective-permute-start | bytes 2064392 | tf_op jit(solution)/shard_map/ppermute | solution.py:101
  98.4 23.9 %collective-permute-start.13 = (bf16[3,64,1792]{2,1,0:T(8,128)(2,1)S(1)}, bf16[3,64,1792]{2,1,0:T(8,128)(2,1)S(1)}, u32[]{:S(2)}, u32[]{:S(2)}) collective-permute-start(bf16[3,64,1792]{2,1,0:T(8,128)(2,1)S(1)} %pad_maximum_fusion.11), channel_id=1, source_target_pairs={{0,8},{8,0},{16,24},{24,16},{1,9},{9,1},{17,25},{25,17},{2,10},{10... | collective-permute-start | bytes 2064392 | tf_op jit(solution)/shard_map/ppermute | solution.py:101
  108.0 14.5 %collective-permute-start.22 = (bf16[3,64,1792]{2,1,0:T(8,128)(2,1)S(1)}, bf16[3,64,1792]{2,1,0:T(8,128)(2,1)S(1)}, u32[]{:S(2)}, u32[]{:S(2)}) collective-permute-start(bf16[3,64,1792]{2,1,0:T(8,128)(2,1)S(1)} %pad_maximum_fusion.12), channel_id=1, source_target_pairs={{0,8},{8,0},{16,24},{24,16},{1,9},{9,1},{17,25},{25,17},{2,10},{10... | collective-permute-start | bytes 2064392 | tf_op jit(solution)/shard_map/ppermute | solution.py:101
  109.5 34.9 %collective-permute-start.36 = (bf16[2,64,1792]{2,1,0:T(8,128)(2,1)S(1)}, bf16[2,64,1792]{2,1,0:T(8,128)(2,1)S(1)}, u32[]{:S(2)}, u32[]{:S(2)}) collective-permute-start(bf16[2,64,1792]{2,1,0:T(8,128)(2,1)S(1)} %pad_maximum_fusion.19), channel_id=1, source_target_pairs={{0,1},{1,0},{2,3},{3,2},{4,5},{5,4},{6,7},{7,6},{8,9},{9,8},{10,11... | collective-permute-start | bytes 1376264 | tf_op jit(solution)/shard_map/ppermute | solution.py:97
  112.7 42.6 %collective-permute-start.31 = (bf16[3,64,1792]{2,1,0:T(8,128)(2,1)S(1)}, bf16[3,64,1792]{2,1,0:T(8,128)(2,1)S(1)}, u32[]{:S(2)}, u32[]{:S(2)}) collective-permute-start(bf16[3,64,1792]{2,1,0:T(8,128)(2,1)S(1)} %pad_maximum_fusion.13), channel_id=1, source_target_pairs={{0,8},{8,0},{16,24},{24,16},{1,9},{9,1},{17,25},{25,17},{2,10},{10... | collective-permute-start | bytes 2064392 | tf_op jit(solution)/shard_map/ppermute | solution.py:101
  121.6 24.2 %collective-permute-start.40 = (bf16[2,64,1792]{2,1,0:T(8,128)(2,1)S(1)}, bf16[2,64,1792]{2,1,0:T(8,128)(2,1)S(1)}, u32[]{:S(2)}, u32[]{:S(2)}) collective-permute-start(bf16[2,64,1792]{2,1,0:T(8,128)(2,1)S(1)} %pad_maximum_fusion.21), channel_id=1, source_target_pairs={{0,1},{1,0},{2,3},{3,2},{4,5},{5,4},{6,7},{7,6},{8,9},{9,8},{10,11... | collective-permute-start | bytes 1376264 | tf_op jit(solution)/shard_map/ppermute | solution.py:97
  122.3 27.7 %collective-permute-start.39 = (bf16[2,64,1792]{2,1,0:T(8,128)(2,1)S(1)}, bf16[2,64,1792]{2,1,0:T(8,128)(2,1)S(1)}, u32[]{:S(2)}, u32[]{:S(2)}) collective-permute-start(bf16[2,64,1792]{2,1,0:T(8,128)(2,1)S(1)} %collective-permute-done.38), channel_id=1, source_target_pairs={{0,8},{8,0},{16,24},{24,16},{1,9},{9,1},{17,25},{25,17},{2,10},{10... | collective-permute-start | bytes 1376264 | tf_op jit(solution)/shard_map/ppermute | solution.py:101
  123.4 20.2 %collective-permute-start.23 = (bf16[64,1024]{1,0:T(8,128)(2,1)S(1)}, bf16[64,1024]{1,0:T(8,128)(2,1)S(1)}, u32[]{:S(2)}, u32[]{:S(2)}) collective-permute-start(bf16[64,1024]{1,0:T(8,128)(2,1)S(1)} %broadcast_select_fusion.11), channel_id=1, source_target_pairs={{0,1},{1,0},{2,3},{3,2},{4,5},{5,4},{6,7},{7,6},{8,9},{9,8},{10,11... | collective-permute-start | bytes 393224 | tf_op jit(solution)/shard_map/ppermute | solution.py:97
  144.4 26.2 %collective-permute-start.6 = (bf16[64,1024]{1,0:T(8,128)(2,1)S(1)}, bf16[64,1024]{1,0:T(8,128)(2,1)S(1)}, u32[]{:S(2)}, u32[]{:S(2)}) collective-permute-start(bf16[64,1024]{1,0:T(8,128)(2,1)S(1)} %broadcast_select_fusion.13), channel_id=1, source_target_pairs={{0,1},{1,0},{2,3},{3,2},{4,5},{5,4},{6,7},{7,6},{8,9},{9,8},{10,11... | collective-permute-start | bytes 393224 | tf_op jit(solution)/shard_map/ppermute | solution.py:97
  150.0 20.5 %collective-permute-start.24 = (bf16[64,1024]{1,0:T(8,128)(2,1)S(1)}, bf16[64,1024]{1,0:T(8,128)(2,1)S(1)}, u32[]{:S(2)}, u32[]{:S(2)}) collective-permute-start(bf16[64,1024]{1,0:T(8,128)(2,1)S(1)} %add_convert_fusion.2), channel_id=1, source_target_pairs={{0,2},{2,4},{4,6},{6,0},{1,3},{3,5},{5,7},{7,1},{8,10},{10,12},{12... | collective-permute-start | bytes 393224 | tf_op jit(solution)/shard_map/ppermute | solution.py:97
  150.5 20.1 %collective-permute-start.15 = (bf16[64,1024]{1,0:T(8,128)(2,1)S(1)}, bf16[64,1024]{1,0:T(8,128)(2,1)S(1)}, u32[]{:S(2)}, u32[]{:S(2)}) collective-permute-start(bf16[64,1024]{1,0:T(8,128)(2,1)S(1)} %add_convert_fusion.3), channel_id=1, source_target_pairs={{0,6},{2,0},{4,2},{6,4},{1,7},{3,1},{5,3},{7,5},{8,14},{10,8},{12,... | collective-permute-start | bytes 393224 | tf_op jit(solution)/shard_map/ppermute | solution.py:97
  (27 other events, 211.3 us)
